TPU v7x, 32 devices: a whole 2x2x4 slice. The times are simulated.
32 devices in a mesh: dp: 8 (over z, x), ctx: 4 (over y, core).
Axes of the slice: x: 2, y: 2, z: 4, core: 2. Of those that a mesh axis runs over, the one named last changes fastest.
Arguments:
- queries: bfloat16 [8, 1024, 2048], P('dp', 'ctx'), may hold values from -100 to 100
- keys: bfloat16 [8, 1024, 512], P('dp', 'ctx'), may hold values from -4 to 4
- values: bfloat16 [8, 1024, 512], P('dp', 'ctx'), may hold values from -6 to 6
- segments: int32 [8, 1024], P('dp', 'ctx'), may hold values from 0 to 7, never falling along the last dimension, each value on 1 to 512 neighbouring positions
Outputs:
- attended: bfloat16 [8, 1024, 2048], P('dp', 'ctx')
Inputs may be any that keep to these rules, and one draw needn't show every extreme that they name: `segments`: document numbers never fall along a packed batch, every one of the 8 documents is present, and each document has at most 512 tokens; some document has exactly 512.
All inputs are finite; a program needn't handle non-finite values.
Results may differ from a plain program's by a relative error of at most 0.0053.
Values may be sent and summed in bfloat16 or wider, within the bound.
A program may use at most 192 MiB of HBM per device.

v0:
```python
import jax
import jax.numpy as jnp
from jax import lax
from jax.sharding import PartitionSpec as P

HQ = 16
HK = 4
HD = 128


rope_theta = 500000.0


def entering(value, axis, join, neutral):
    count, mine = (lax.axis_size(axis), lax.axis_index(axis))
    pieces = jax.tree.map(lambda part: lax.all_gather(part, axis), value)
    running = jax.tree.map(
        lambda part, zero: jnp.full_like(part, 0) + jnp.asarray(zero, part.dtype), value, neutral
    )

    def hop(position, running):
        longer = join(running, jax.tree.map(lambda part: part[position], pieces))
        return jax.tree.map(lambda new, old: jnp.where(position < mine, new, old), longer, running)

    return lax.fori_loop(0, count - 1, hop, running)


def from_behind(block, axis, distance):
    devices = range(lax.axis_size(axis))
    route = [(i - distance, i) for i in devices if i - distance in devices]
    return lax.ppermute(block, axis, route)


def rotate(values_in, positions, heads, head_dim):
    rows = values_in.shape[0]
    half_dim = head_dim // 2
    split = values_in.astype(jnp.float32).reshape(rows, heads, head_dim)
    inv_freq = jnp.exp(
        -jnp.log(rope_theta) * 2.0 * jnp.arange(half_dim, dtype=jnp.float32) / head_dim
    )
    angles = positions.astype(jnp.float32)[:, None] * inv_freq[None, :]
    cosine_part = jnp.cos(angles)[:, None, :]
    sine_part = jnp.sin(angles)[:, None, :]
    first_half = split[..., :half_dim]
    second_half = split[..., half_dim:]
    turned = jnp.concatenate(
        [
            first_half * cosine_part - second_half * sine_part,
            second_half * cosine_part + first_half * sine_part,
        ],
        axis=-1,
    )
    return turned.reshape(rows, heads * head_dim).astype(jnp.bfloat16)


def join_runs(earlier, later):
    joined_uniform = earlier[3] * later[3] * (earlier[1] == later[0]).astype(jnp.int32)
    joined_trail = jnp.where(
        (later[3] == 1) & (later[0] == earlier[1]), earlier[2] + later[2], later[2]
    )
    joined = (earlier[0], later[1], joined_trail, joined_uniform, jnp.int32(0))
    return tuple(
        (
            jnp.where(
                earlier[4] == 1, later_part, jnp.where(later[4] == 1, earlier_part, joined_part)
            )
            for earlier_part, later_part, joined_part in zip(earlier, later, joined)
        )
    )


def attend_piece(
    state_in, key_piece, value_piece, key_segs, key_start, query_heads, query_segs, query_index
):
    run_max, run_sum, accumulated = state_in
    width = key_piece.shape[0]
    kv_heads = query_heads.shape[1]
    head_dim = query_heads.shape[3]
    key_heads = key_piece.reshape(width, kv_heads, head_dim)
    value_heads = value_piece.reshape(width, kv_heads, head_dim)
    key_index = key_start + jnp.arange(width, dtype=jnp.int32)
    live_mask = (
        (key_segs[None, :] == query_segs[:, None])
        & (key_index[None, :] <= query_index[:, None])
        & (key_index[None, :] >= 0)
    )
    scores = jnp.einsum(
        "thgd,shd->hgts", query_heads, key_heads, preferred_element_type=jnp.float32
    ) / jnp.sqrt(jnp.float32(head_dim))
    scores = jnp.where(live_mask, scores, jnp.float32(-1e30))
    new_max = jnp.maximum(run_max, jnp.max(scores, axis=-1))
    weights = jnp.where(live_mask, jnp.exp(scores - new_max[..., None]), jnp.float32(0.0))
    rescale = jnp.exp(run_max - new_max)
    new_sum = run_sum * rescale + jnp.sum(weights, axis=-1)
    weighted = jnp.einsum(
        "hgts,shd->thgd",
        weights.astype(jnp.bfloat16),
        value_heads,
        preferred_element_type=jnp.float32,
    )
    new_acc = accumulated * jnp.transpose(rescale, (2, 0, 1))[..., None] + weighted
    return (new_max, new_sum, new_acc)


def body(queries, keys, values, segments):
    tok_rows = segments.shape[1]
    cycle_size = lax.axis_size("ctx")
    cycle_index = lax.axis_index("ctx")
    seg_ids = segments[0]
    index_all = jnp.arange(tok_rows, dtype=jnp.int32)
    previous = jnp.concatenate([seg_ids[:1] - 1, seg_ids[:-1]])
    run_start = lax.cummax(jnp.where(seg_ids != previous, index_all, 0), axis=0)
    local_pos = index_all - run_start
    summary = (
        seg_ids[0],
        seg_ids[-1],
        jnp.int32(tok_rows) - run_start[-1],
        (seg_ids[0] == seg_ids[-1]).astype(jnp.int32),
        jnp.int32(0),
    )
    identity = (jnp.int32(0), jnp.int32(0), jnp.int32(0), jnp.int32(1), jnp.int32(1))
    prefix = entering(summary, "ctx", join_runs, identity)
    carried = jnp.where((prefix[4] == 0) & (prefix[1] == seg_ids[0]), prefix[2], 0)
    positions = jnp.where(run_start == 0, local_pos + carried, local_pos)
    head_dim = HD
    q_heads_all = HQ
    kv_heads = HK
    group_size = q_heads_all // kv_heads
    rot_q = rotate(queries[0], positions, q_heads_all, head_dim)
    rot_k = rotate(keys[0], positions, kv_heads, head_dim)
    query_heads = rot_q.reshape(tok_rows, kv_heads, group_size, head_dim)
    query_index = cycle_index * tok_rows + index_all
    initial = (
        jnp.full((kv_heads, group_size, tok_rows), -1e30, jnp.float32),
        jnp.zeros((kv_heads, group_size, tok_rows), jnp.float32),
        jnp.zeros((tok_rows, kv_heads, group_size, head_dim), jnp.float32),
    )
    own_state = attend_piece(
        initial,
        rot_k,
        values[0],
        seg_ids,
        cycle_index * tok_rows,
        query_heads,
        seg_ids,
        query_index,
    )

    def pass_step(step_index, loop_state):
        state_now, travelling = loop_state
        arrived = from_behind((travelling[0], travelling[1], travelling[2]), "ctx", 1)
        updated = attend_piece(
            state_now,
            arrived[0],
            arrived[1],
            arrived[2],
            (cycle_index - step_index) * tok_rows,
            query_heads,
            seg_ids,
            query_index,
        )
        return (updated, arrived)

    final_state, unused_piece = lax.fori_loop(
        1, cycle_size // 2 + 1, pass_step, (own_state, (rot_k, values[0], seg_ids))
    )
    run_max, run_sum, accumulated = final_state
    result = accumulated / jnp.transpose(run_sum, (2, 0, 1))[..., None]
    attended = result.reshape(tok_rows, q_heads_all * head_dim).astype(jnp.bfloat16)[None]
    return attended


def solution(mesh):
    placed = (P("dp", "ctx", None), P("dp", "ctx", None), P("dp", "ctx", None), P("dp", "ctx"))
    return jax.shard_map(
        body, mesh=mesh, in_specs=placed, out_specs=P("dp", "ctx", None), check_vma=False
    )
```

profile of v0, /device:TPU:1, one launch (start us, length us, event | category | flops | bytes accessed | tf_op | source)
XLA Modules:
  0.0 91.6 jit_solution(15335493625381826933)
XLA Ops:
  0.0 1.3 %fusion.41 = (s32[1,1]{1,0:T(1,128)}, s32[1,1]{1,0:T(1,128)}) fusion(s32[1,256]{1,0:T(1,128)} %param.11), kind=kLoop, calls=%fused_computation.70 | loop fusion | bytes 16 | tf_op jit(solution)/shard_map/slice | solution.py:116
  2.0 0.8 compare_select_fusion.1
  3.4 1.3 %dynamic-slice = u32[1]{0:T(128)} dynamic-slice(u32[32]{0:T(128)} %constant.119, u32[]{:T(128)S(6)} %add.134), dynamic_slice_sizes={1} | dynamic-slice | bytes 12
  4.7 0.8 subtract_dynamic-update-slice_fusion
  6.7 0.7 dynamic-update-slice.3
  7.5 1.3 %bitcast_dynamic-update-slice_fusion = s32[4]{0:T(128)S(1)} fusion(s32[4]{0:T(128)S(1)} %broadcast.133.clone.4, u32[]{:T(128)} %bitcast.13, s32[1,1]{1,0:T(1,128)} %get-tuple-element.457), kind=kLoop, calls=%fused_computation.60 | loop fusion | bytes 24
  8.8 1.2 %bitcast_dynamic-update-slice_fusion.1 = s32[4]{0:T(128)S(1)} fusion(s32[4]{0:T(128)S(1)} %broadcast.133.clone, u32[]{:T(128)} %bitcast.13, s32[1,1]{1,0:T(1,128)} %get-tuple-element.456), kind=kLoop, calls=%fused_computation.61 | loop fusion | bytes 24
  10.1 0.7 dynamic-update-slice.1
  10.8 5.1 %all-reduce.5 = (s32[4]{0:T(128)S(1)}, s32[4]{0:T(128)S(1)}, s32[4]{0:T(128)S(1)}, s32[4]{0:T(128)S(1)}, s32[4]{0:T(128)S(1)}) all-reduce(s32[4]{0:T(128)S(1)} %bitcast_dynamic-update-slice_fusion.1, s32[4]{0:T(128)S(1)} %dynamic-update-slice.1, s32[4]{0:T(128)S(1)} %subtract_dynamic-update-slice_fusion, ...), channel_id=2, replica_groups=mesh['dp'=8,'ctx'=4] {'ctx'}, use_global_device_ids=true, to_apply=%add | all-reduce | flops 20 | bytes 160 | tf_op jit(solution)/shard_map/all_gather | solution.py:16
  15.9 24.0 %while.41 = (s32[]{:T(128)}, s32[]{:T(128)}, s32[]{:T(128)}, s32[]{:T(128)}, s32[]{:T(128)}, /*index=5*/s32[4]{0:T(128)S(1)}, s32[4]{0:T(128)S(1)}, s32[4]{0:T(1...) while((s32[]{:T(128)}, s32[]{:T(128)}, s32[]{:T(128)}, s32[]{:T(128)}, ...), condition=%wide.region_3.4_spmd, body=%wide.region_2.3_spmd.sunk | while | flops 19 | bytes 375 | solution.py:25
  17.0 0.6 dynamic_slice.43
  18.2 0.6 dynamic_slice.42
  19.9 0.6 dynamic_slice.41
  25.1 0.6 dynamic_slice.43
  26.2 0.6 dynamic_slice.42
  27.9 0.6 dynamic_slice.41
  33.1 0.6 dynamic_slice.43
  34.2 0.6 dynamic_slice.42
  35.9 0.6 dynamic_slice.41
  41.2 1.5 %convert_bitcast_fusion = f32[32,8,16,128]{3,1,2,0:T(8,128)S(1)} fusion(bf16[1,256,2048]{2,1,0:T(8,128)(2,1)} %param.8), kind=kLoop, calls=%fused_computation.30 | loop fusion | flops 524288 | bytes 3145728
  43.1 0.7 fusion.39
  43.8 1.4 %subtract_convert_fusion = (bf16[256,16,64]{2,0,1:T(8,128)(2,1)S(1)}, bf16[256,16,64]{2,0,1:T(8,128)(2,1)S(1)}) fusion(f32[256,16,64]{2,1,0:T(8,128)S(1)} %get-tuple-element.447, f32[256,16,64]{2,1,0:T(8,128)S(1)} %get-tuple-element.446, f32[256,64]{1,0:T(8,128)S(1)} %get-tuple-element.455, f32[256,64]{1,0:T(8,128)S(1)} %get-tuple-element.454), kind=kLoop, calls=%fused_computation.37 | loop fusion | flops 2097152 | bytes 3276800 | tf_op jit(solution)/shard_map/convert.3
  46.9 0.8 fusion.18
  47.7 1.9 %copy-done = f32[4,256,256,4]{2,1,3,0:T(8,128)} copy-done((f32[4,256,256,4]{2,1,3,0:T(8,128)}, f32[4,256,256,4]{2,1,3,0:T(8,128)S(1)}, u32[]{:S(2)}) %copy-start) | copy-done | bytes 4194328
  49.6 1.0 %fusion.20 = f32[4,4,256]{2,1,0:T(4,128)S(1)} fusion(f32[4,256,256,4]{2,1,3,0:T(8,128)S(1)} %get-tuple-element.459, f32[4,4,256]{2,1,0:T(4,128)S(1)} %broadcast_maximum_fusion, pred[256,256]{0,1:T(8,128)(4,1)S(1)} %and_and_fusion.1), kind=kLoop, calls=%fused_computation.27 | loop fusion | flops 5238784 | bytes 4292608 | tf_op jit(solution)/shard_map/reduce_sum | solution.py:94
  50.7 5.3 %bitcast_add_fusion.1 = f32[256,4,4,128]{3,0,2,1:T(8,128)} fusion(f32[4,256,256,4]{2,1,3,0:T(8,128)} %copy-done, f32[4,4,256]{2,1,0:T(4,128)S(1)} %broadcast_maximum_fusion, pred[256,256]{0,1:T(8,128)(4,1)S(1)} %and_and_fusion.1, f32[256,4,4]{0,2,1:T(4,128)S(1)} %get-tuple-element.452, bf16[256,4,128,1]{2,1,0,3:T(4,128)(2,1)S(1)} %bitcast.152), kind=kOutput, calls=%fused_computation.29 | convolution fusion | flops 274202624 | bytes 6651904 | tf_op jit(solution)/shard_map/hgts,shd->thgd/dot_general | solution.py:95
  56.3 30.9 %while.42 = (s32[]{:T(128)}, f32[4,4,256]{2,1,0:T(4,128)S(1)}, f32[4,4,256]{2,1,0:T(4,128)S(1)}, f32[256,4,4,128]{3,0,2,1:T(8,128)}, bf16[256,512]{0,1:T(8,128)(...) while((s32[]{:T(128)}, f32[4,4,256]{2,1,0:T(4,128)S(1)}, ...), condition=%wide.region_9.10_spmd.clone, body=%wide.region_6.9_spmd.clone.sunk | while | flops 551826432 | bytes 38810448 | solution.py:164
  56.5 3.7 %collective-permute-start = (s32[256]{0:T(256)S(1)}, s32[256]{0:T(256)S(1)}, u32[]{:S(2)}, u32[]{:S(2)}) collective-permute-start(s32[256]{0:T(256)S(1)} %get-tuple-element.658), channel_id=1, source_target_pairs={{0,1},{1,2},{2,3},{4,5},{5,6},{6,7},{8,9},{9,10},{10,11},{12,13},{... | collective-permute-start | bytes 3080 | tf_op jit(solution)/shard_map/while/body/eval_jaxpr/ppermute | solution.py:31
  60.2 1.9 %collective-permute-start.1 = (bf16[256,512]{0,1:T(8,128)(2,1)S(1)}, bf16[256,512]{0,1:T(8,128)(2,1)S(1)}, u32[]{:S(2)}, u32[]{:S(2)}) collective-permute-start(bf16[256,512]{0,1:T(8,128)(2,1)S(1)} %get-tuple-element.656), channel_id=1, source_target_pairs={{0,1},{1,2},{2,3},{4,5},{5,6},{6,7},{8,9},{9,10},{10,11},{12,13},{... | collective-permute-start | bytes 786440 | tf_op jit(solution)/shard_map/while/body/eval_jaxpr/ppermute | solution.py:31
  62.1 1.9 %collective-permute-start.2 = (bf16[256,512]{0,1:T(8,128)(2,1)S(1)}, bf16[256,512]{0,1:T(8,128)(2,1)S(1)}, u32[]{:S(2)}, u32[]{:S(2)}) collective-permute-start(bf16[256,512]{0,1:T(8,128)(2,1)S(1)} %get-tuple-element.657), channel_id=1, source_target_pairs={{0,1},{1,2},{2,3},{4,5},{5,6},{6,7},{8,9},{9,10},{10,11},{12,13},{... | collective-permute-start | bytes 786440 | tf_op jit(solution)/shard_map/while/body/eval_jaxpr/ppermute | solution.py:31
  64.3 1.1 %collective-permute-done.1 = bf16[256,512]{0,1:T(8,128)(2,1)S(1)} collective-permute-done((bf16[256,512]{0,1:T(8,128)(2,1)S(1)}, bf16[256,512]{0,1:T(8,128)(2,1)S(1)}, u32[]{:S(2)}, u32[]{:S(2)}) %collective-permute-start.1) | collective-permute-done | bytes 262176 | tf_op jit(solution)/shard_map/while/body/eval_jaxpr/ppermute | solution.py:31
  65.4 0.9 fusion.57
  66.3 1.0 %fusion.59 = f32[4,4,256]{2,1,0:T(4,128)S(1)} fusion(f32[4,256,256,4]{2,1,3,0:T(8,128)S(1)} %get-tuple-element.598, f32[4,4,256]{2,1,0:T(4,128)S(1)} %get-tuple-element.666, pred[256,256]{0,1:T(8,128)(4,1)S(1)} %and_and_fusion.3), kind=kLoop, calls=%fused_computation.5.clone.1 | loop fusion | flops 5238784 | bytes 4292608 | tf_op jit(solution)/shard_map/while/body/eval_jaxpr/reduce_sum | solution.py:94
  67.4 0.8 collective-permute-done.2
  68.2 1.9 %bitcast_add_fusion.3 = f32[256,4,4,128]{3,0,2,1:T(8,128)S(1)} fusion(f32[256,4,4,128]{3,0,2,1:T(8,128)S(1)} %copy-done.1, bf16[256,4,128,1]{0,2,3,1:T(8,128)(2,1)S(1)} %bitcast.143, f32[4,256,256,4]{2,1,3,0:T(8,128)S(1)} %get-tuple-element.598, f32[4,4,256]{2,1,0:T(4,128)S(1)} %get-tuple-element.666, pred[256,256]{0,1:T(8,128)(4,1)S(1)} %and_and_fusion.3, ...), kind=kOutput, calls=%fused_computation.7.clone.1 | convolution fusion | flops 274726912 | bytes 8749056 | tf_op jit(solution)/shard_map/while/body/eval_jaxpr/hgts,shd->thgd/dot_general | solution.py:95
  70.2 1.3 %copy-done.2 = f32[256,4,4,128]{3,0,2,1:T(8,128)} copy-done((f32[256,4,4,128]{3,0,2,1:T(8,128)}, f32[256,4,4,128]{3,0,2,1:T(8,128)S(1)}, u32[]{:S(2)}) %copy-start.2) | copy-done | bytes 2097176 | tf_op jit(solution)/shard_map/while
  71.5 4.4 %collective-permute-start = (s32[256]{0:T(256)S(1)}, s32[256]{0:T(256)S(1)}, u32[]{:S(2)}, u32[]{:S(2)}) collective-permute-start(s32[256]{0:T(256)S(1)} %get-tuple-element.658), channel_id=1, source_target_pairs={{0,1},{1,2},{2,3},{4,5},{5,6},{6,7},{8,9},{9,10},{10,11},{12,13},{... | collective-permute-start | bytes 3080 | tf_op jit(solution)/shard_map/while/body/eval_jaxpr/ppermute | solution.py:31
  75.9 1.9 %collective-permute-start.1 = (bf16[256,512]{0,1:T(8,128)(2,1)S(1)}, bf16[256,512]{0,1:T(8,128)(2,1)S(1)}, u32[]{:S(2)}, u32[]{:S(2)}) collective-permute-start(bf16[256,512]{0,1:T(8,128)(2,1)S(1)} %get-tuple-element.656), channel_id=1, source_target_pairs={{0,1},{1,2},{2,3},{4,5},{5,6},{6,7},{8,9},{9,10},{10,11},{12,13},{... | collective-permute-start | bytes 786440 | tf_op jit(solution)/shard_map/while/body/eval_jaxpr/ppermute | solution.py:31
  77.8 1.9 %collective-permute-start.2 = (bf16[256,512]{0,1:T(8,128)(2,1)S(1)}, bf16[256,512]{0,1:T(8,128)(2,1)S(1)}, u32[]{:S(2)}, u32[]{:S(2)}) collective-permute-start(bf16[256,512]{0,1:T(8,128)(2,1)S(1)} %get-tuple-element.657), channel_id=1, source_target_pairs={{0,1},{1,2},{2,3},{4,5},{5,6},{6,7},{8,9},{9,10},{10,11},{12,13},{... | collective-permute-start | bytes 786440 | tf_op jit(solution)/shard_map/while/body/eval_jaxpr/ppermute | solution.py:31
  80.0 1.1 %collective-permute-done.1 = bf16[256,512]{0,1:T(8,128)(2,1)S(1)} collective-permute-done((bf16[256,512]{0,1:T(8,128)(2,1)S(1)}, bf16[256,512]{0,1:T(8,128)(2,1)S(1)}, u32[]{:S(2)}, u32[]{:S(2)}) %collective-permute-start.1) | collective-permute-done | bytes 262176 | tf_op jit(solution)/shard_map/while/body/eval_jaxpr/ppermute | solution.py:31
  81.1 0.9 fusion.57
  82.0 1.0 %fusion.59 = f32[4,4,256]{2,1,0:T(4,128)S(1)} fusion(f32[4,256,256,4]{2,1,3,0:T(8,128)S(1)} %get-tuple-element.598, f32[4,4,256]{2,1,0:T(4,128)S(1)} %get-tuple-element.666, pred[256,256]{0,1:T(8,128)(4,1)S(1)} %and_and_fusion.3), kind=kLoop, calls=%fused_computation.5.clone.1 | loop fusion | flops 5238784 | bytes 4292608 | tf_op jit(solution)/shard_map/while/body/eval_jaxpr/reduce_sum | solution.py:94
  83.1 0.8 collective-permute-done.2
  83.9 1.9 %bitcast_add_fusion.3 = f32[256,4,4,128]{3,0,2,1:T(8,128)S(1)} fusion(f32[256,4,4,128]{3,0,2,1:T(8,128)S(1)} %copy-done.1, bf16[256,4,128,1]{0,2,3,1:T(8,128)(2,1)S(1)} %bitcast.143, f32[4,256,256,4]{2,1,3,0:T(8,128)S(1)} %get-tuple-element.598, f32[4,4,256]{2,1,0:T(4,128)S(1)} %get-tuple-element.666, pred[256,256]{0,1:T(8,128)(4,1)S(1)} %and_and_fusion.3, ...), kind=kOutput, calls=%fused_computation.7.clone.1 | convolution fusion | flops 274726912 | bytes 8749056 | tf_op jit(solution)/shard_map/while/body/eval_jaxpr/hgts,shd->thgd/dot_general | solution.py:95
  85.9 1.3 %copy-done.2 = f32[256,4,4,128]{3,0,2,1:T(8,128)} copy-done((f32[256,4,4,128]{3,0,2,1:T(8,128)}, f32[256,4,4,128]{3,0,2,1:T(8,128)S(1)}, u32[]{:S(2)}) %copy-start.2) | copy-done | bytes 2097176 | tf_op jit(solution)/shard_map/while
  87.2 1.9 %divide_convert_fusion = bf16[256,4,4,128]{3,0,2,1:T(8,128)(2,1)S(1)} fusion(f32[256,4,4,128]{3,0,2,1:T(8,128)} %get-tuple-element.364, f32[256,4,4]{0,2,1:T(4,128)S(1)} %bitcast.149), kind=kLoop, calls=%fused_computation.31 | loop fusion | flops 1048576 | bytes 3162112 | tf_op jit(solution)/shard_map/convert_element_type | solution.py:169
  89.1 0.8 copy.23
  89.9 1.6 %convert_element_type.68 = bf16[1,256,2048]{2,1,0:T(8,128)(2,1)} reshape(bf16[256,4,4,128]{3,2,1,0:T(4,128)(2,1)S(1)} %copy.23) | data formatting | bytes 2097152 | tf_op jit(solution)/shard_map/convert_element_type | solution.py:169
  (69 shorter events, 7.6 us)
Async XLA Ops:
  43.7 2.0 %copy-start.4 = (bf16[1,256,512]{2,1,0:T(8,128)(2,1)S(1)}, bf16[1,256,512]{2,1,0:T(8,128)(2,1)}, u32[]{:S(2)}) copy-start(bf16[1,256,512]{2,1,0:T(8,128)(2,1)} %param.9) | copy-start | bytes 786436
  45.1 1.5 %copy-start.5 = (s32[1,256]{1,0:T(1,128)S(1)}, s32[1,256]{1,0:T(1,128)}, u32[]{:S(2)}) copy-start(s32[1,256]{1,0:T(1,128)} %param.11) | copy-start | bytes 3076
  46.8 3.8 %copy-start.3 = (bf16[1,256,512]{2,1,0:T(8,128)(2,1)S(1)}, bf16[1,256,512]{2,1,0:T(8,128)(2,1)}, u32[]{:S(2)}) copy-start(bf16[1,256,512]{2,1,0:T(8,128)(2,1)} %param.10) | copy-start | bytes 786436
  47.6 1.9 %copy-start = (f32[4,256,256,4]{2,1,3,0:T(8,128)}, f32[4,256,256,4]{2,1,3,0:T(8,128)S(1)}, u32[]{:S(2)}) copy-start(f32[4,256,256,4]{2,1,3,0:T(8,128)S(1)} %get-tuple-element.459) | copy-start | bytes 12582916
  56.5 7.6 %collective-permute-start = (s32[256]{0:T(256)S(1)}, s32[256]{0:T(256)S(1)}, u32[]{:S(2)}, u32[]{:S(2)}) collective-permute-start(s32[256]{0:T(256)S(1)} %get-tuple-element.658), channel_id=1, source_target_pairs={{0,1},{1,2},{2,3},{4,5},{5,6},{6,7},{8,9},{9,10},{10,11},{12,13},{... | collective-permute-start | bytes 3080 | tf_op jit(solution)/shard_map/while/body/eval_jaxpr/ppermute | solution.py:31
  60.2 5.2 %collective-permute-start.1 = (bf16[256,512]{0,1:T(8,128)(2,1)S(1)}, bf16[256,512]{0,1:T(8,128)(2,1)S(1)}, u32[]{:S(2)}, u32[]{:S(2)}) collective-permute-start(bf16[256,512]{0,1:T(8,128)(2,1)S(1)} %get-tuple-element.656), channel_id=1, source_target_pairs={{0,1},{1,2},{2,3},{4,5},{5,6},{6,7},{8,9},{9,10},{10,11},{12,13},{... | collective-permute-start | bytes 786440 | tf_op jit(solution)/shard_map/while/body/eval_jaxpr/ppermute | solution.py:31
  62.1 6.1 %collective-permute-start.2 = (bf16[256,512]{0,1:T(8,128)(2,1)S(1)}, bf16[256,512]{0,1:T(8,128)(2,1)S(1)}, u32[]{:S(2)}, u32[]{:S(2)}) collective-permute-start(bf16[256,512]{0,1:T(8,128)(2,1)S(1)} %get-tuple-element.657), channel_id=1, source_target_pairs={{0,1},{1,2},{2,3},{4,5},{5,6},{6,7},{8,9},{9,10},{10,11},{12,13},{... | collective-permute-start | bytes 786440 | tf_op jit(solution)/shard_map/while/body/eval_jaxpr/ppermute | solution.py:31
  65.4 2.8 %copy-start.1 = (f32[256,4,4,128]{3,0,2,1:T(8,128)S(1)}, f32[256,4,4,128]{3,0,2,1:T(8,128)}, u32[]{:S(2)}) copy-start(f32[256,4,4,128]{3,0,2,1:T(8,128)} %get-tuple-element.655) | copy-start | bytes 6291460 | tf_op jit(solution)/shard_map/while
  70.2 1.3 %copy-start.2 = (f32[256,4,4,128]{3,0,2,1:T(8,128)}, f32[256,4,4,128]{3,0,2,1:T(8,128)S(1)}, u32[]{:S(2)}) copy-start(f32[256,4,4,128]{3,0,2,1:T(8,128)S(1)} %bitcast_add_fusion.3) | copy-start | bytes 6291460 | tf_op jit(solution)/shard_map/while
  71.5 8.3 %collective-permute-start = (s32[256]{0:T(256)S(1)}, s32[256]{0:T(256)S(1)}, u32[]{:S(2)}, u32[]{:S(2)}) collective-permute-start(s32[256]{0:T(256)S(1)} %get-tuple-element.658), channel_id=1, source_target_pairs={{0,1},{1,2},{2,3},{4,5},{5,6},{6,7},{8,9},{9,10},{10,11},{12,13},{... | collective-permute-start | bytes 3080 | tf_op jit(solution)/shard_map/while/body/eval_jaxpr/ppermute | solution.py:31
  75.9 5.2 %collective-permute-start.1 = (bf16[256,512]{0,1:T(8,128)(2,1)S(1)}, bf16[256,512]{0,1:T(8,128)(2,1)S(1)}, u32[]{:S(2)}, u32[]{:S(2)}) collective-permute-start(bf16[256,512]{0,1:T(8,128)(2,1)S(1)} %get-tuple-element.656), channel_id=1, source_target_pairs={{0,1},{1,2},{2,3},{4,5},{5,6},{6,7},{8,9},{9,10},{10,11},{12,13},{... | collective-permute-start | bytes 786440 | tf_op jit(solution)/shard_map/while/body/eval_jaxpr/ppermute | solution.py:31
  77.8 6.1 %collective-permute-start.2 = (bf16[256,512]{0,1:T(8,128)(2,1)S(1)}, bf16[256,512]{0,1:T(8,128)(2,1)S(1)}, u32[]{:S(2)}, u32[]{:S(2)}) collective-permute-start(bf16[256,512]{0,1:T(8,128)(2,1)S(1)} %get-tuple-element.657), channel_id=1, source_target_pairs={{0,1},{1,2},{2,3},{4,5},{5,6},{6,7},{8,9},{9,10},{10,11},{12,13},{... | collective-permute-start | bytes 786440 | tf_op jit(solution)/shard_map/while/body/eval_jaxpr/ppermute | solution.py:31
  81.1 2.8 %copy-start.1 = (f32[256,4,4,128]{3,0,2,1:T(8,128)S(1)}, f32[256,4,4,128]{3,0,2,1:T(8,128)}, u32[]{:S(2)}) copy-start(f32[256,4,4,128]{3,0,2,1:T(8,128)} %get-tuple-element.655) | copy-start | bytes 6291460 | tf_op jit(solution)/shard_map/while
  85.8 1.3 %copy-start.2 = (f32[256,4,4,128]{3,0,2,1:T(8,128)}, f32[256,4,4,128]{3,0,2,1:T(8,128)S(1)}, u32[]{:S(2)}) copy-start(f32[256,4,4,128]{3,0,2,1:T(8,128)S(1)} %bitcast_add_fusion.3) | copy-start | bytes 6291460 | tf_op jit(solution)/shard_map/while
where the time goes:
time: 92.2 us; the launch traced here: 91.6 us
  local copies, waits for them, and re-layouts  24.4 us (26%)
  loops' own time  15.8 us (17%)
  starting transfers between devices  15.8 us (17%)
  other arithmetic  12 us (13%)
  matrix products  11.7 us (13%)
  blocking collectives  5.07 us (5%)
  waiting for transfers between devices  3.95 us (4%)
  between operations  2.94 us (3%)
    ppermute x6, starting transfers between devices, from_behind(): return lax.ppermute(block, axis, route)  15.8 us
    another operation x1, loops' own time, entering(): return lax.fori_loop(0, count - 1, hop, running)  15.3 us
    dot_general x3, matrix products, attend_piece(): jnp.einsum('hgts,shd->thgd', weights.astype(jnp.bfloat16), value_heads, p...  9.11 us
    dynamic_slice x15, local copies, waits for them, and re-layouts, hop(): longer = join(running, jax.tree.map(lambda part: part[position], pieces))  8.71 us
    unnamed x24, local copies, waits for them, and re-layouts  8.3 us
    all_gather x1, blocking collectives, entering(): pieces = jax.tree.map(lambda part: lax.all_gather(part, axis), value)  5.07 us
    ppermute x6, waiting for transfers between devices, from_behind(): return lax.ppermute(block, axis, route)  3.95 us
    reduce_sum x3, other arithmetic, attend_piece(): new_sum = run_sum * rescale + jnp.sum(weights, axis=-1)  3.11 us
  transfers between devices with their start and end apart: 6, of which 4 were waited for; matrix products, arithmetic and copies ran while one was open for 5% of the time, Pallas kernels for 0%

commit v1 on v0

v1 whole, which is shorter than its diff:
```python
import functools
import math

import jax
import jax.numpy as jnp
from jax import lax
from jax.experimental import pallas as pl
from jax.experimental.pallas import tpu as pltpu
from jax.sharding import PartitionSpec as P

HK = 4
HD = 128
THETA = 500000.0
LANES = 128
MASKED = -1e30
F32 = jnp.float32
BF16 = jnp.bfloat16


def sin_cos(angle):
    turns = jnp.floor(angle * (2.0 / math.pi) + 0.5)
    rest = angle - turns * 1.5703125
    rest = rest - turns * 4.837512969970703125e-4
    rest = rest - turns * 7.54978995489188216e-8
    square = rest * rest
    sine = rest + rest * square * (
        -1.6666654611e-1 + square * (8.3321608736e-3 + square * -1.9515295891e-4)
    )
    cosine = (
        1.0
        - 0.5 * square
        + square * square * (4.166664568298827e-2 + square * (-1.388731625493765e-3 + square * 2.443315711809948e-5))
    )
    quarter = turns - 4.0 * jnp.floor(turns * 0.25)
    odd = (quarter == 1.0) | (quarter == 3.0)
    sin_out = jnp.where(odd, cosine, sine)
    cos_out = jnp.where(odd, sine, cosine)
    sin_out = jnp.where(quarter >= 2.0, -sin_out, sin_out)
    cos_out = jnp.where((quarter == 1.0) | (quarter == 2.0), -cos_out, cos_out)
    return sin_out, cos_out


def frequencies():
    index = lax.broadcasted_iota(jnp.int32, (1, HD), 1) % (HD // 2)
    result = jnp.ones((1, HD), F32)
    bit = 1
    while bit < HD // 2:
        factor = math.exp(-math.log(THETA) * 2.0 * bit / HD)
        result = result * jnp.where((index // bit) % 2 == 1, F32(factor), F32(1.0))
        bit *= 2
    return result


def turned(block, cosine, sine):
    block = block.astype(F32)
    return (block * cosine + pltpu.roll(block, HD // 2, 1) * sine).astype(BF16)


def kernel(
    count, hops, q_ref, k_ref, v_ref, seg_ref, out_ref,
    q_own, kwin, vwin, segwin, krot, qrot, weights, denoms, sines, cosines, bias,
    q_sem, seg_sem, own_sem, seg_send, seg_recv, send, recv, forward,
):
    me = lax.axis_index("ctx")
    rows = q_own.shape[0]
    width = kwin.shape[1]
    group = qrot.shape[0] // HK
    windows = (kwin, vwin)

    def block(which, head, distance):
        return windows[which].at[head, pl.ds((hops - distance) * rows, rows)]

    own_copies = [
        [
            pltpu.make_async_copy(
                ref.at[0, :, pl.ds(head * HD, HD)], block(which, head, 0), own_sem.at[which, head]
            )
            for head in range(HK)
        ]
        for which, ref in enumerate((k_ref, v_ref))
    ]
    seg_copy = pltpu.make_async_copy(seg_ref, segwin.at[hops], seg_sem)
    q_copy = pltpu.make_async_copy(q_ref.at[0], q_own, q_sem)
    seg_copy.start()
    for head in range(HK):
        for which in range(2):
            own_copies[which][head].start()
    q_copy.start()

    barrier = pltpu.get_barrier_semaphore()
    for distance in range(1, hops + 1):
        @pl.when(me + distance < count)
        def _():
            pl.semaphore_signal(barrier, inc=1, device_id={"ctx": me + distance})

        @pl.when(me >= distance)
        def _():
            pl.semaphore_signal(barrier, inc=1, device_id={"ctx": me - distance})
    pl.semaphore_wait(barrier, jnp.minimum(me, hops) + jnp.minimum(count - 1 - me, hops))

    def seg_out(distance):
        return pltpu.make_async_remote_copy(
            src_ref=segwin.at[hops], dst_ref=segwin.at[hops - distance],
            send_sem=seg_send.at[distance - 1], recv_sem=seg_recv.at[distance - 1],
            device_id={"ctx": me + distance},
        )

    def block_out(which, head, distance):
        return pltpu.make_async_remote_copy(
            src_ref=block(which, head, 0), dst_ref=block(which, head, distance),
            send_sem=send.at[which, head, distance - 1], recv_sem=recv.at[which, head, distance - 1],
            device_id={"ctx": me + distance},
        )

    def block_on(which, head, distance):
        return pltpu.make_async_remote_copy(
            src_ref=block(which, head, distance), dst_ref=block(which, head, distance + 1),
            send_sem=forward.at[which, head, distance - 1], recv_sem=recv.at[which, head, distance],
            device_id={"ctx": me + 1},
        )

    def goes_out(distance):
        direct = me + distance < count
        if distance > 1:
            direct = direct & ((me + distance) % 2 == 0)
        return direct

    def goes_on(distance):
        return (me % 2 == 0) & (me >= distance) & (me + 1 < count)

    seg_copy.wait()
    for distance in range(1, hops + 1):
        @pl.when(me + distance < count)
        def _():
            seg_out(distance).start()
    for head in range(HK):
        for which in range(2):
            own_copies[which][head].wait()
            for distance in range(hops, 0, -1):
                @pl.when(goes_out(distance))
                def _():
                    block_out(which, head, distance).start()

    for distance in range(1, hops + 1):
        @pl.when(me < distance)
        def _():
            empty = jnp.zeros((HK, rows, HD), BF16)
            kwin[:, pl.ds((hops - distance) * rows, rows)] = empty
            vwin[:, pl.ds((hops - distance) * rows, rows)] = empty
            segwin[hops - distance] = jnp.full((1, rows), -1, jnp.int32)

    for distance in range(1, hops + 1):
        @pl.when(me >= distance)
        def _():
            seg_out(distance).wait_recv()

    freq = frequencies()
    lane = lax.broadcasted_iota(jnp.int32, (rows, LANES), 1)
    row = lax.broadcasted_iota(jnp.int32, (rows, LANES), 0)
    sign = jnp.where(lane < HD // 2, F32(-1.0), F32(1.0))
    ones = jnp.ones((LANES, LANES), BF16)
    pieces = []
    for index in range(hops + 1):
        seg_row = segwin[index].astype(F32)
        pieces += [seg_row[:, at:at + LANES] for at in range(0, rows, LANES)]
    for index in range(hops + 1):
        column = jnp.broadcast_to(segwin[index].astype(F32), (LANES, rows)).T
        smaller = jnp.zeros((rows, LANES), F32)
        for piece in pieces:
            smaller = smaller + jnp.where(piece < column, F32(1.0), F32(0.0))
        start = jnp.dot(smaller.astype(BF16), ones, preferred_element_type=F32)
        position = (row + index * rows).astype(F32) - start
        sine, cosine = sin_cos(position * freq)
        sines[index] = sine * sign
        cosines[index] = cosine
        if index == hops:
            last = (row + hops * rows).astype(F32)
            for at in range(0, width, LANES):
                spot = (lane + at).astype(F32)
                bias[:, at:at + LANES] = jnp.where(
                    (spot >= start) & (spot <= last), F32(0.0), F32(MASKED)
                )

    q_copy.wait()

    @pl.loop(0, qrot.shape[0])
    def _(head):
        at = pl.ds(pl.multiple_of(head * HD, HD), HD)
        qrot[head] = turned(q_own[:, at], cosines[hops], sines[hops])

    scale = F32(math.log2(math.e) / math.sqrt(HD))

    def arrive(which, head):
        for distance in range(1, hops + 1):
            @pl.when(me >= distance)
            def _():
                block_out(which, head, distance).wait_recv()
            if distance < hops:
                @pl.when(goes_on(distance))
                def _():
                    block_on(which, head, distance).start()

    @pl.loop(0, HK)
    def _(head):
        arrive(0, head)
        for index in range(hops + 1):
            at = pl.ds(index * rows, rows)
            krot[at] = turned(kwin[head, at], cosines[index], sines[index])

        @pl.loop(0, group)
        def _(part):
            scores = lax.dot_general(
                qrot[head * group + part], krot[...], (((1,), (1,)), ((), ())),
                preferred_element_type=F32,
            ) + bias[...]
            top = jnp.max(scores, axis=1, keepdims=True)
            weight = jnp.exp2((scores - top) * scale)
            denoms[part] = jnp.broadcast_to(jnp.sum(weight, axis=1, keepdims=True), (rows, LANES))
            weights[part] = weight.astype(BF16)

        arrive(1, head)

        @pl.loop(0, group)
        def _(part):
            total = jnp.dot(weights[part], vwin[head], preferred_element_type=F32)
            at = pl.ds(pl.multiple_of((head * group + part) * HD, HD), HD)
            out_ref[0, :, at] = (total / denoms[part]).astype(BF16)

    for distance in range(1, hops + 1):
        @pl.when(me + distance < count)
        def _():
            seg_out(distance).wait_send()
        for which in range(2):
            for head in range(HK):
                @pl.when(goes_out(distance))
                def _():
                    block_out(which, head, distance).wait_send()
                if distance < hops:
                    @pl.when(goes_on(distance))
                    def _():
                        block_on(which, head, distance).wait_send()


def body(queries, keys, values, segments):
    count = lax.axis_size("ctx")
    hops = count // 2
    rows = queries.shape[1]
    width = (hops + 1) * rows
    heads = queries.shape[2] // HD
    group = heads // HK
    anywhere = pl.BlockSpec(memory_space=pltpu.HBM)
    dma = pltpu.SemaphoreType.DMA
    return pl.pallas_call(
        functools.partial(kernel, count, hops),
        out_shape=jax.ShapeDtypeStruct(queries.shape, BF16),
        in_specs=[anywhere] * 4,
        out_specs=pl.BlockSpec(memory_space=pltpu.VMEM),
        scratch_shapes=[
            pltpu.VMEM((rows, heads * HD), BF16),
            pltpu.VMEM((HK, width, HD), BF16),
            pltpu.VMEM((HK, width, HD), BF16),
            pltpu.VMEM((hops + 1, 1, rows), jnp.int32),
            pltpu.VMEM((width, HD), BF16),
            pltpu.VMEM((heads, rows, HD), BF16),
            pltpu.VMEM((group, rows, width), BF16),
            pltpu.VMEM((group, rows, LANES), F32),
            pltpu.VMEM((hops + 1, rows, HD), F32),
            pltpu.VMEM((hops + 1, rows, HD), F32),
            pltpu.VMEM((rows, width), F32),
            dma, dma, dma((2, HK)),
            dma((hops,)), dma((hops,)),
            dma((2, HK, hops)), dma((2, HK, hops)), dma((2, HK, hops)),
        ],
        compiler_params=pltpu.CompilerParams(
            collective_id=0, has_side_effects=True, vmem_limit_bytes=48 * 1024 * 1024
        ),
        name="attend",
    )(queries, keys, values, segments)


def solution(mesh):
    placed = (P("dp", "ctx", None), P("dp", "ctx", None), P("dp", "ctx", None), P("dp", "ctx"))
    return jax.shard_map(
        body, mesh=mesh, in_specs=placed, out_specs=P("dp", "ctx", None), check_vma=False
    )
```

time: 92.2 us -> 25.5 us (0.28)
  the two profiles are of different devices: /device:TPU:1 before, /device:TPU:21 now
where the time goes in v1:
time: 25.5 us; the launch traced here: 25.3 us
  Pallas kernels  20.5 us (80%)
  local copies, waits for them, and re-layouts  4.77 us (19%)
    pallas_call x1, Pallas kernels, body(): pl.pallas_call(functools.partial(kernel, count, hops), out_shape=jax.Shap...  20.5 us
    unnamed x9, local copies, waits for them, and re-layouts  4.77 us

profile of v1, /device:TPU:21, one launch (start us, length us, event | category | flops | bytes accessed | tf_op | source)
XLA Modules:
  0.0 25.3 jit_solution(11607406871636934599)
XLA Ops:
  0.0 0.0 copy-start
  0.0 1.2 %copy-done = bf16[1,256,2048]{2,1,0:T(8,128)(2,1)S(1)} copy-done((bf16[1,256,2048]{2,1,0:T(8,128)(2,1)S(1)}, bf16[1,256,2048]{2,1,0:T(8,128)(2,1)}, u32[]{:S(2)}) %copy-start) | copy-done | bytes 1048600
  1.2 0.0 copy-start.1
  1.2 0.9 %copy-done.1 = bf16[1,256,512]{2,1,0:T(8,128)(2,1)S(1)} copy-done((bf16[1,256,512]{2,1,0:T(8,128)(2,1)S(1)}, bf16[1,256,512]{2,1,0:T(8,128)(2,1)}, u32[]{:S(2)}) %copy-start.1) | copy-done | bytes 262168
  2.2 0.0 copy-start.2
  2.2 0.9 %copy-done.2 = bf16[1,256,512]{2,1,0:T(8,128)(2,1)S(1)} copy-done((bf16[1,256,512]{2,1,0:T(8,128)(2,1)S(1)}, bf16[1,256,512]{2,1,0:T(8,128)(2,1)}, u32[]{:S(2)}) %copy-start.2) | copy-done | bytes 262168
  3.1 0.0 copy-start.3
  3.1 0.7 %copy-done.3 = s32[1,256]{1,0:T(1,128)S(1)} copy-done((s32[1,256]{1,0:T(1,128)S(1)}, s32[1,256]{1,0:T(1,128)}, u32[]{:S(2)}) %copy-start.3) | copy-done | bytes 1048
  3.8 20.5 %attend.1 = bf16[1,256,2048]{2,1,0:T(8,128)(2,1)S(1)} custom-call(bf16[1,256,2048]{2,1,0:T(8,128)(2,1)S(1)} %copy-done, bf16[1,256,512]{2,1,0:T(8,128)(2,1)S(1)} %copy-done.1, bf16[1,256,512]{2,1,0:T(8,128)(2,1)S(1)} %copy-done.2, s32[1,256]{1,0:T(1,128)S(1)} %copy-done.3), custom_call_target="tpu_custom_call" | custom-call | tf_op jit(solution)/shard_map/attend/pallas_call | solution.py:253
  24.3 1.0 %copy.6 = bf16[1,256,2048]{2,1,0:T(8,128)(2,1)} copy(bf16[1,256,2048]{2,1,0:T(8,128)(2,1)S(1)} %attend.1) | data formatting | bytes 2097152
Async XLA Ops:
  0.0 1.2 %copy-start = (bf16[1,256,2048]{2,1,0:T(8,128)(2,1)S(1)}, bf16[1,256,2048]{2,1,0:T(8,128)(2,1)}, u32[]{:S(2)}) copy-start(bf16[1,256,2048]{2,1,0:T(8,128)(2,1)} %q_ref.1) | copy-start | bytes 3145732
  1.2 0.9 %copy-start.1 = (bf16[1,256,512]{2,1,0:T(8,128)(2,1)S(1)}, bf16[1,256,512]{2,1,0:T(8,128)(2,1)}, u32[]{:S(2)}) copy-start(bf16[1,256,512]{2,1,0:T(8,128)(2,1)} %k_ref.1) | copy-start | bytes 786436
  2.2 0.9 %copy-start.2 = (bf16[1,256,512]{2,1,0:T(8,128)(2,1)S(1)}, bf16[1,256,512]{2,1,0:T(8,128)(2,1)}, u32[]{:S(2)}) copy-start(bf16[1,256,512]{2,1,0:T(8,128)(2,1)} %v_ref.1) | copy-start | bytes 786436
  3.1 0.7 %copy-start.3 = (s32[1,256]{1,0:T(1,128)S(1)}, s32[1,256]{1,0:T(1,128)}, u32[]{:S(2)}) copy-start(s32[1,256]{1,0:T(1,128)} %seg_ref.1) | copy-start | bytes 3076

commit v2 on v1

--- a/solution.py
+++ b/solution.py
@@ -63,7 +63,7 @@
 ):
     me = lax.axis_index("ctx")
     rows = q_own.shape[0]
-    width = kwin.shape[1]
+    span = bias.shape[2]
     group = qrot.shape[0] // HK
     windows = (kwin, vwin)
 
@@ -136,9 +136,17 @@
     for head in range(HK):
         for which in range(2):
             own_copies[which][head].wait()
-            for distance in range(hops, 0, -1):
-                @pl.when(goes_out(distance))
-                def _():
+
+            @pl.when(goes_out(1))
+            def _():
+                block_out(which, head, 1).start()
+    for distance in range(2, hops + 1):
+        @pl.when(goes_out(distance))
+        def _():
+            for head in range(HK):
+                for which in range(2):
+                    if distance == 2:
+                        block_out(which, head, 1).wait_send()
                     block_out(which, head, distance).start()
 
     for distance in range(1, hops + 1):
@@ -175,11 +183,13 @@
         cosines[index] = cosine
         if index == hops:
             last = (row + hops * rows).astype(F32)
-            for at in range(0, width, LANES):
-                spot = (lane + at).astype(F32)
-                bias[:, at:at + LANES] = jnp.where(
-                    (spot >= start) & (spot <= last), F32(0.0), F32(MASKED)
-                )
+            for tile in range(rows // LANES):
+                mine = slice(tile * LANES, (tile + 1) * LANES)
+                for at in range(0, span, LANES):
+                    spot = (lane[mine] + (at + tile * LANES)).astype(F32)
+                    bias[tile, :, at:at + LANES] = jnp.where(
+                        (spot >= start[mine]) & (spot <= last[mine]), F32(0.0), F32(MASKED)
+                    )
 
     q_copy.wait()
 
@@ -190,49 +200,60 @@
 
     scale = F32(math.log2(math.e) / math.sqrt(HD))
 
-    def arrive(which, head):
-        for distance in range(1, hops + 1):
-            @pl.when(me >= distance)
+    def arrive(head, distance, which):
+        @pl.when(me >= distance)
+        def _():
+            block_out(which, head, distance).wait_recv()
+        if distance < hops:
+            @pl.when(goes_on(distance))
             def _():
-                block_out(which, head, distance).wait_recv()
-            if distance < hops:
-                @pl.when(goes_on(distance))
-                def _():
-                    block_on(which, head, distance).start()
+                block_on(which, head, distance).start()
 
     @pl.loop(0, HK)
     def _(head):
-        arrive(0, head)
+        for distance in range(1, hops):
+            for which in range(2):
+                arrive(head, distance, which)
+        arrive(head, hops, 0)
         for index in range(hops + 1):
             at = pl.ds(index * rows, rows)
             krot[at] = turned(kwin[head, at], cosines[index], sines[index])
 
-        @pl.loop(0, group)
-        def _(part):
-            scores = lax.dot_general(
-                qrot[head * group + part], krot[...], (((1,), (1,)), ((), ())),
-                preferred_element_type=F32,
-            ) + bias[...]
-            top = jnp.max(scores, axis=1, keepdims=True)
-            weight = jnp.exp2((scores - top) * scale)
-            denoms[part] = jnp.broadcast_to(jnp.sum(weight, axis=1, keepdims=True), (rows, LANES))
-            weights[part] = weight.astype(BF16)
-
-        arrive(1, head)
-
-        @pl.loop(0, group)
-        def _(part):
-            total = jnp.dot(weights[part], vwin[head], preferred_element_type=F32)
-            at = pl.ds(pl.multiple_of((head * group + part) * HD, HD), HD)
-            out_ref[0, :, at] = (total / denoms[part]).astype(BF16)
+        for part in range(group):
+            for tile in range(rows // LANES):
+                mine = slice(tile * LANES, (tile + 1) * LANES)
+                seen = pl.ds(tile * LANES, span)
+                scores = lax.dot_general(
+                    qrot[head * group + part, mine], krot[seen], (((1,), (1,)), ((), ())),
+                    preferred_element_type=F32,
+                ) + bias[tile]
+                top = jnp.max(scores, axis=1, keepdims=True)
+                weight = jnp.exp2((scores - top) * scale)
+                denoms[part, mine] = jnp.broadcast_to(
+                    jnp.sum(weight, axis=1, keepdims=True), (LANES, LANES)
+                )
+                weights[part, mine] = weight.astype(BF16)
+
+        arrive(head, hops, 1)
+
+        for part in range(group):
+            for tile in range(rows // LANES):
+                mine = slice(tile * LANES, (tile + 1) * LANES)
+                seen = pl.ds(tile * LANES, span)
+                total = jnp.dot(weights[part, mine], vwin[head, seen], preferred_element_type=F32)
+                at = pl.ds(pl.multiple_of((head * group + part) * HD, HD), HD)
+                out_ref[0, mine, at] = (total / denoms[part, mine]).astype(BF16)
 
     for distance in range(1, hops + 1):
         @pl.when(me + distance < count)
         def _():
             seg_out(distance).wait_send()
+        unsent = goes_out(distance)
+        if distance == 1 and hops > 1:
+            unsent = unsent & jnp.logical_not(goes_out(2))
         for which in range(2):
             for head in range(HK):
-                @pl.when(goes_out(distance))
+                @pl.when(unsent)
                 def _():
                     block_out(which, head, distance).wait_send()
                 if distance < hops:
@@ -246,6 +267,7 @@
     hops = count // 2
     rows = queries.shape[1]
     width = (hops + 1) * rows
+    span = hops * rows + LANES
     heads = queries.shape[2] // HD
     group = heads // HK
     anywhere = pl.BlockSpec(memory_space=pltpu.HBM)
@@ -262,17 +284,17 @@
             pltpu.VMEM((hops + 1, 1, rows), jnp.int32),
             pltpu.VMEM((width, HD), BF16),
             pltpu.VMEM((heads, rows, HD), BF16),
-            pltpu.VMEM((group, rows, width), BF16),
+            pltpu.VMEM((group, rows, span), BF16),
             pltpu.VMEM((group, rows, LANES), F32),
             pltpu.VMEM((hops + 1, rows, HD), F32),
             pltpu.VMEM((hops + 1, rows, HD), F32),
-            pltpu.VMEM((rows, width), F32),
+            pltpu.VMEM((rows // LANES, LANES, span), F32),
             dma, dma, dma((2, HK)),
             dma((hops,)), dma((hops,)),
             dma((2, HK, hops)), dma((2, HK, hops)), dma((2, HK, hops)),
         ],
         compiler_params=pltpu.CompilerParams(
-            collective_id=0, has_side_effects=True, vmem_limit_bytes=48 * 1024 * 1024
+            collective_id=0, has_side_effects=True, vmem_limit_bytes=63 * 1024 * 1024
         ),
         name="attend",
     )(queries, keys, values, segments)

time: 25.5 us -> 20.4 us (0.80)
  Pallas kernels: 20.5 us -> 18 us
  local copies, waits for them, and re-layouts: 4.77 us -> 2.3 us
    pallas_call x1, Pallas kernels: 20.5 us -> 18 us  [body(): pl.pallas_call(functools.partial(kernel, count, hops), out_shape=jax.Shap...]
    unnamed x9 -> x1, local copies, waits for them, and re-layouts: 4.77 us -> 2.3 us
where the time goes in v2:
time: 20.4 us; the launch traced here: 20.3 us
  Pallas kernels  18 us (88%)
  local copies, waits for them, and re-layouts  2.3 us (11%)
    pallas_call x1, Pallas kernels, body(): pl.pallas_call(functools.partial(kernel, count, hops), out_shape=jax.Shap...  18 us
    unnamed x1, local copies, waits for them, and re-layouts  2.3 us

profile of v2, /device:TPU:21, one launch (start us, length us, event | category | flops | bytes accessed | tf_op | source)
XLA Modules:
  0.0 20.3 jit_solution(3865685730826707739)
XLA Ops:
  0.0 18.0 %attend.1 = bf16[1,256,2048]{2,1,0:T(8,128)(2,1)} custom-call(bf16[1,256,2048]{2,1,0:T(8,128)(2,1)} %q_ref.1, bf16[1,256,512]{2,1,0:T(8,128)(2,1)} %k_ref.1, bf16[1,256,512]{2,1,0:T(8,128)(2,1)} %v_ref.1, s32[1,256]{1,0:T(1,128)} %seg_ref.1), custom_call_target="tpu_custom_call" | custom-call | tf_op jit(solution)/shard_map/attend/pallas_call | solution.py:275
  18.0 2.3 %copy.6 = bf16[1,256,2048]{2,1,0:T(8,128)(2,1)} copy(bf16[1,256,2048]{2,1,0:T(8,128)(2,1)} %attend.1) | data formatting | bytes 2097152

commit v3 on v2

--- a/solution.py
+++ b/solution.py
@@ -82,8 +82,8 @@
     seg_copy = pltpu.make_async_copy(seg_ref, segwin.at[hops], seg_sem)
     q_copy = pltpu.make_async_copy(q_ref.at[0], q_own, q_sem)
     seg_copy.start()
-    for head in range(HK):
-        for which in range(2):
+    for which in range(2):
+        for head in range(HK):
             own_copies[which][head].start()
     q_copy.start()
 
@@ -133,8 +133,8 @@
         @pl.when(me + distance < count)
         def _():
             seg_out(distance).start()
-    for head in range(HK):
-        for which in range(2):
+    for which in range(2):
+        for head in range(HK):
             own_copies[which][head].wait()
 
             @pl.when(goes_out(1))
@@ -143,8 +143,8 @@
     for distance in range(2, hops + 1):
         @pl.when(goes_out(distance))
         def _():
-            for head in range(HK):
-                for which in range(2):
+            for which in range(2):
+                for head in range(HK):
                     if distance == 2:
                         block_out(which, head, 1).wait_send()
                     block_out(which, head, distance).start()
@@ -211,10 +211,8 @@
 
     @pl.loop(0, HK)
     def _(head):
-        for distance in range(1, hops):
-            for which in range(2):
-                arrive(head, distance, which)
-        arrive(head, hops, 0)
+        for distance in range(1, hops + 1):
+            arrive(head, distance, 0)
         for index in range(hops + 1):
             at = pl.ds(index * rows, rows)
             krot[at] = turned(kwin[head, at], cosines[index], sines[index])
@@ -229,10 +227,20 @@
                 ) + bias[tile]
                 top = jnp.max(scores, axis=1, keepdims=True)
                 weight = jnp.exp2((scores - top) * scale)
-                denoms[part, mine] = jnp.broadcast_to(
+                denoms[head * group + part, mine] = jnp.broadcast_to(
                     jnp.sum(weight, axis=1, keepdims=True), (LANES, LANES)
                 )
-                weights[part, mine] = weight.astype(BF16)
+                weights[head * group + part, mine] = weight.astype(BF16)
+
+    for distance in range(1, hops):
+        arrive(0, distance, 1)
+
+    @pl.loop(0, HK)
+    def _(head):
+        @pl.when(head + 1 < HK)
+        def _():
+            for distance in range(1, hops):
+                arrive(head + 1, distance, 1)
 
         arrive(head, hops, 1)
 
@@ -240,9 +248,9 @@
             for tile in range(rows // LANES):
                 mine = slice(tile * LANES, (tile + 1) * LANES)
                 seen = pl.ds(tile * LANES, span)
-                total = jnp.dot(weights[part, mine], vwin[head, seen], preferred_element_type=F32)
+                total = jnp.dot(weights[head * group + part, mine], vwin[head, seen], preferred_element_type=F32)
                 at = pl.ds(pl.multiple_of((head * group + part) * HD, HD), HD)
-                out_ref[0, mine, at] = (total / denoms[part, mine]).astype(BF16)
+                out_ref[0, mine, at] = (total / denoms[head * group + part, mine]).astype(BF16)
 
     for distance in range(1, hops + 1):
         @pl.when(me + distance < count)
@@ -274,7 +282,7 @@
     dma = pltpu.SemaphoreType.DMA
     return pl.pallas_call(
         functools.partial(kernel, count, hops),
-        out_shape=jax.ShapeDtypeStruct(queries.shape, BF16),
+        out_shape=pltpu.VMEM(queries.shape, BF16),
         in_specs=[anywhere] * 4,
         out_specs=pl.BlockSpec(memory_space=pltpu.VMEM),
         scratch_shapes=[
@@ -284,8 +292,8 @@
             pltpu.VMEM((hops + 1, 1, rows), jnp.int32),
             pltpu.VMEM((width, HD), BF16),
             pltpu.VMEM((heads, rows, HD), BF16),
-            pltpu.VMEM((group, rows, span), BF16),
-            pltpu.VMEM((group, rows, LANES), F32),
+            pltpu.VMEM((heads, rows, span), BF16),
+            pltpu.VMEM((heads, rows, LANES), F32),
             pltpu.VMEM((hops + 1, rows, HD), F32),
             pltpu.VMEM((hops + 1, rows, HD), F32),
             pltpu.VMEM((rows // LANES, LANES, span), F32),
@@ -294,7 +302,7 @@
             dma((2, HK, hops)), dma((2, HK, hops)), dma((2, HK, hops)),
         ],
         compiler_params=pltpu.CompilerParams(
-            collective_id=0, has_side_effects=True, vmem_limit_bytes=63 * 1024 * 1024
+            collective_id=0, has_side_effects=True, vmem_limit_bytes=60 * 1024 * 1024
         ),
         name="attend",
     )(queries, keys, values, segments)

time: 20.4 us -> 17.1 us (0.84)
  Pallas kernels: 18 us -> 15.9 us
  local copies, waits for them, and re-layouts: 2.3 us -> 0.97 us
    pallas_call x1, Pallas kernels: 18 us -> 15.9 us  [body(): pl.pallas_call(functools.partial(kernel, count, hops), out_shape=pltpu.VM...]
    unnamed x1, local copies, waits for them, and re-layouts: 2.3 us -> 0.97 us
where the time goes in v3:
time: 17.1 us; the launch traced here: 16.9 us
  Pallas kernels  15.9 us (93%)
  local copies, waits for them, and re-layouts  0.97 us (6%)
    pallas_call x1, Pallas kernels, body(): pl.pallas_call(functools.partial(kernel, count, hops), out_shape=pltpu.VM...  15.9 us
    unnamed x1, local copies, waits for them, and re-layouts  0.97 us

profile of v3, /device:TPU:21, one launch (start us, length us, event | category | flops | bytes accessed | tf_op | source)
XLA Modules:
  0.0 16.9 jit_solution(3045473593503038852)
XLA Ops:
  0.0 15.9 %attend.1 = bf16[1,256,2048]{2,1,0:T(8,128)(2,1)S(1)} custom-call(bf16[1,256,2048]{2,1,0:T(8,128)(2,1)} %q_ref.1, bf16[1,256,512]{2,1,0:T(8,128)(2,1)} %k_ref.1, bf16[1,256,512]{2,1,0:T(8,128)(2,1)} %v_ref.1, s32[1,256]{1,0:T(1,128)} %seg_ref.1), custom_call_target="tpu_custom_call" | custom-call | tf_op jit(solution)/shard_map/attend/pallas_call | solution.py:283
  15.9 1.0 %copy.6 = bf16[1,256,2048]{2,1,0:T(8,128)(2,1)} copy(bf16[1,256,2048]{2,1,0:T(8,128)(2,1)S(1)} %attend.1) | data formatting | bytes 2097152

commit v4 on v3

--- a/solution.py
+++ b/solution.py
@@ -143,10 +143,12 @@
     for distance in range(2, hops + 1):
         @pl.when(goes_out(distance))
         def _():
+            if distance == 2:
+                for which in range(2):
+                    for head in range(HK):
+                        block_out(which, head, 1).wait_send()
             for which in range(2):
                 for head in range(HK):
-                    if distance == 2:
-                        block_out(which, head, 1).wait_send()
                     block_out(which, head, distance).start()
 
     for distance in range(1, hops + 1):

time: 17.1 us -> 17.1 us (level)
  no operation moved by 1% of the time
where the time goes in v4:
time: 17.1 us; the launch traced here: 16.9 us
  Pallas kernels  16 us (94%)
  local copies, waits for them, and re-layouts  0.97 us (6%)
    pallas_call x1, Pallas kernels, body(): pl.pallas_call(functools.partial(kernel, count, hops), out_shape=pltpu.VM...  16 us
    unnamed x1, local copies, waits for them, and re-layouts  0.97 us

profile of v4, /device:TPU:21, one launch (start us, length us, event | category | flops | bytes accessed | tf_op | source)
XLA Modules:
  0.0 16.9 jit_solution(17849708493393568364)
XLA Ops:
  0.0 16.0 %attend.1 = bf16[1,256,2048]{2,1,0:T(8,128)(2,1)S(1)} custom-call(bf16[1,256,2048]{2,1,0:T(8,128)(2,1)} %q_ref.1, bf16[1,256,512]{2,1,0:T(8,128)(2,1)} %k_ref.1, bf16[1,256,512]{2,1,0:T(8,128)(2,1)} %v_ref.1, s32[1,256]{1,0:T(1,128)} %seg_ref.1), custom_call_target="tpu_custom_call" | custom-call | tf_op jit(solution)/shard_map/attend/pallas_call | solution.py:285
  16.0 1.0 %copy.6 = bf16[1,256,2048]{2,1,0:T(8,128)(2,1)} copy(bf16[1,256,2048]{2,1,0:T(8,128)(2,1)S(1)} %attend.1) | data formatting | bytes 2097152
